TPU v7x, 32 devices: a whole 2x2x4 slice. The times are simulated.
32 devices in a mesh: seq: 8 (over z, y), head: 4 (over x, core).
Axes of the slice: x: 2, y: 2, z: 4, core: 2. Of those that a mesh axis runs over, the one named last changes fastest.
Arguments:
- queries: bfloat16 [6144, 4096], P(('seq', 'head')), may hold values from -6 to 6
- key_rows: bfloat16 [6144, 4096], P(('seq', 'head')), may hold values from -6 to 6
- values: bfloat16 [6144, 4096], P(('seq', 'head')), may hold values from -6 to 6
- doc_ids: int32 [6144], replicated, may hold values from 0 to 15, as said below
- image_flags: int32 [6144], replicated, may hold values from 0 to 1, as said below
- labels: int32 [6144], P(('seq', 'head')), may hold values from -1 to 31999, as said below
- token_loss: float32 [6144], P(('seq', 'head')), may hold values from 0.05 to 8
Outputs:
- attended: bfloat16 [6144, 4096], P(('seq', 'head'))
- doc_count: float32 [16], replicated
- doc_loss: float32 [16], replicated
Inputs may be any that keep to these rules, and one draw needn't show every extreme that they name: `doc_ids`: document numbers never fall along the sequence and rise by one from one document to the next; every document holds at least 64 and at most 704 tokens, and some document holds exactly 704. `image_flags`: the 1s form spans of exactly 576 consecutive tokens, at most one span a document, each inside one document and never at its first token. `labels`: every image token has -1, and some document has -1 on all of its tokens.
All inputs are finite; a program needn't handle non-finite values.
Results may differ from a plain program's by a relative error of at most 0.0034.
Values may be sent and summed in bfloat16 or wider, within the bound.
No kernel may reach another device: no remote copies, remote signals or barrier semaphores. Data moves between devices by JAX's collectives and lax.ppermute only.
A program may use at most 128 MiB of HBM per device.

v0:
```python
import jax
import jax.numpy as jnp
from jax import lax
from jax.sharding import PartitionSpec as P

HEAD_DIM = 128
TOK_DEV = 768
DOC_MEAN = 384
DOC_MOST = 704
IMG_LEN = 576


def shifted(block, axis, distance):
    devices = range(lax.axis_size(axis))
    route = [(i - distance, i) for i in devices if i - distance in devices]
    return lax.ppermute(block, axis, route)


def cut_rows(reach):
    return min(TOK_DEV, -(-reach // 128) * 128)


def allowed_pairs(query_docs, query_flags, query_places, key_docs, key_flags, key_places):
    same = query_docs[:, None] == key_docs[None, :]
    earlier = key_places[None, :] <= query_places[:, None]
    image = (query_flags[:, None] == 1) & (key_flags[None, :] == 1)
    return same & (earlier | image)


def attend(query_part, key_window, value_window, allowed):
    outputs = []
    scale = HEAD_DIM ** (-0.5)
    for head_index in range(query_part.shape[1] // HEAD_DIM):
        lower = head_index * HEAD_DIM
        query_head = query_part[:, lower : lower + HEAD_DIM]
        key_head = key_window[:, lower : lower + HEAD_DIM]
        value_head = value_window[:, lower : lower + HEAD_DIM]
        scores = (
            lax.dot_general(
                query_head, key_head, (((1,), (1,)), ((), ())), preferred_element_type=jnp.float32
            )
            * scale
        )
        scores = jnp.where(allowed, scores, -jnp.inf)
        row_max = jnp.max(scores, axis=1, keepdims=True)
        weights = jnp.exp(scores - row_max)
        total = jnp.sum(weights, axis=1, keepdims=True)
        mixed = (
            jnp.dot(weights.astype(jnp.bfloat16), value_head, preferred_element_type=jnp.float32)
            / total
        )
        outputs.append(mixed.astype(jnp.bfloat16))
    return jnp.concatenate(outputs, axis=1)


def per_device(queries, key_rows, values, doc_ids, image_flags, labels, token_loss):
    query_local, key_local, value_local = (
        lax.all_to_all(queries, "head", split_axis=1, concat_axis=0, tiled=True),
        lax.all_to_all(key_rows, "head", split_axis=1, concat_axis=0, tiled=True),
        lax.all_to_all(values, "head", split_axis=1, concat_axis=0, tiled=True),
    )
    reach_back = (DOC_MOST + TOK_DEV - 2) // TOK_DEV
    reach_front = (IMG_LEN + TOK_DEV - 2) // TOK_DEV
    behind = [shifted((key_local, value_local), "seq", 1)]
    ahead = [
        shifted(
            (
                key_local[: cut_rows(IMG_LEN - 1 - (1 - 1) * TOK_DEV)],
                value_local[: cut_rows(IMG_LEN - 1 - (1 - 1) * TOK_DEV)],
            ),
            "seq",
            -1,
        )
    ]
    key_window = jnp.concatenate(
        [pair[0] for pair in behind] + [key_local] + [pair[0] for pair in ahead], axis=0
    )
    value_window = jnp.concatenate(
        [pair[1] for pair in behind] + [value_local] + [pair[1] for pair in ahead], axis=0
    )
    back_total = sum((pair[0].shape[0] for pair in behind))
    window_rows = key_window.shape[0]
    block_start = lax.axis_index("seq") * TOK_DEV
    pad_front = reach_back * TOK_DEV
    pad_back = reach_front * TOK_DEV
    padded_docs = jnp.pad(doc_ids, (pad_front, pad_back), constant_values=-1)
    padded_flags = jnp.pad(image_flags, (pad_front, pad_back))
    key_docs = lax.dynamic_slice_in_dim(
        padded_docs, block_start + pad_front - back_total, window_rows
    )
    key_flags = lax.dynamic_slice_in_dim(
        padded_flags, block_start + pad_front - back_total, window_rows
    )
    query_docs = lax.dynamic_slice_in_dim(doc_ids, block_start, TOK_DEV)
    query_flags = lax.dynamic_slice_in_dim(image_flags, block_start, TOK_DEV)
    query_places = block_start + jnp.arange(TOK_DEV, dtype=jnp.int32)
    key_places = block_start - back_total + jnp.arange(window_rows, dtype=jnp.int32)
    allowed = allowed_pairs(query_docs, query_flags, query_places, key_docs, key_flags, key_places)
    attended = attend(query_local, key_window, value_window, allowed)
    output = lax.all_to_all(attended, "head", split_axis=0, concat_axis=1, tiled=True)
    local_rows = labels.shape[0]
    row_start = (
        lax.axis_index("seq") * lax.axis_size("head") + lax.axis_index("head")
    ) * local_rows
    local_docs = lax.dynamic_slice_in_dim(doc_ids, row_start, local_rows)
    documents = doc_ids.shape[0] // DOC_MEAN
    member = (local_docs[:, None] == jnp.arange(documents, dtype=jnp.int32)[None, :]) & (
        labels[:, None] >= 0
    )
    counts = jnp.sum(member.astype(jnp.float32), axis=0)
    sums = jnp.sum(jnp.where(member, token_loss[:, None], jnp.float32(0.0)), axis=0)
    counts, sums = lax.psum((counts, sums), ("seq", "head"))
    return (output, counts, sums / jnp.maximum(counts, jnp.float32(1.0)))


def solution(mesh):
    in_specs = (
        P(("seq", "head"), None),
        P(("seq", "head"), None),
        P(("seq", "head"), None),
        P(),
        P(),
        P(("seq", "head")),
        P(("seq", "head")),
    )
    out_specs = (P(("seq", "head"), None), P(), P())
    return jax.shard_map(
        per_device, mesh=mesh, in_specs=in_specs, out_specs=out_specs, check_vma=False
    )
```

profile of v0, /device:TPU:0, one launch (start us, length us, event | category | flops | bytes accessed | tf_op | source)
XLA Modules:
  0.0 272.2 jit_solution(8038829767457793462)
XLA Ops:
  3.5 4.2 %all-to-all-start = ((bf16[192,4,1024]{2,0,1:T(8,128)(2,1)}), bf16[192,4,1024]{2,0,1:T(8,128)(2,1)S(1)}, u32[]{:S(2)}, u32[]{:S(2)}) async-start(bf16[192,4,1024]{2,0,1:T(8,128)(2,1)} %bitcast.40), calls=%async_computation | async-start | bytes 3145728 | tf_op jit(solution)/shard_map/all_to_all | solution.py:59
  9.0 18.7 %all-to-all-done = bf16[192,4,1024]{2,0,1:T(8,128)(2,1)S(1)} async-done(((bf16[192,4,1024]{2,0,1:T(8,128)(2,1)}), bf16[192,4,1024]{2,0,1:T(8,128)(2,1)S(1)}, u32[]{:S(2)}, u32[]{:S(2)}) %all-to-all-start) | async-done | bytes 1572896 | tf_op jit(solution)/shard_map/all_to_all | solution.py:59
  27.7 3.6 %all-to-all-start.2 = ((bf16[192,4,1024]{2,0,1:T(8,128)(2,1)}), bf16[192,4,1024]{2,0,1:T(8,128)(2,1)S(1)}, u32[]{:S(2)}, u32[]{:S(2)}) async-start(bf16[192,4,1024]{2,0,1:T(8,128)(2,1)} %bitcast.53), calls=%async_computation.2 | async-start | bytes 3145728 | tf_op jit(solution)/shard_map/all_to_all | solution.py:60
  31.3 5.4 %collective-permute-start = (bf16[768,1024]{1,0:T(8,128)(2,1)S(1)}, bf16[768,1024]{1,0:T(8,128)(2,1)}, u32[]{:S(2)}, u32[]{:S(2)}) collective-permute-start(bf16[768,1024]{1,0:T(8,128)(2,1)S(1)} %bitcast.44), channel_id=1, source_target_pairs={{0,4},{4,8},{8,12},{12,16},{16,20},{20,24},{24,28},{1,5},{5,9},{9,... | collective-permute-start | bytes 4718600 | tf_op jit(solution)/shard_map/ppermute | solution.py:16
  41.9 9.4 %all-to-all-done.2 = bf16[192,4,1024]{2,0,1:T(8,128)(2,1)S(1)} async-done(((bf16[192,4,1024]{2,0,1:T(8,128)(2,1)}), bf16[192,4,1024]{2,0,1:T(8,128)(2,1)S(1)}, u32[]{:S(2)}, u32[]{:S(2)}) %all-to-all-start.2) | async-done | bytes 1572896 | tf_op jit(solution)/shard_map/all_to_all | solution.py:60
  51.3 4.3 %all-to-all-start.1 = ((bf16[192,4,1024]{2,0,1:T(8,128)(2,1)}), bf16[192,4,1024]{2,0,1:T(8,128)(2,1)}, u32[]{:S(2)}, u32[]{:S(2)}) async-start(bf16[192,4,1024]{2,0,1:T(8,128)(2,1)} %bitcast.51), calls=%async_computation.1 | async-start | bytes 3145728 | tf_op jit(solution)/shard_map/all_to_all | solution.py:58
  57.2 5.3 %collective-permute-start.2 = (bf16[768,1024]{1,0:T(8,128)(2,1)S(1)}, bf16[768,1024]{1,0:T(8,128)(2,1)}, u32[]{:S(2)}, u32[]{:S(2)}) collective-permute-start(bf16[768,1024]{1,0:T(8,128)(2,1)S(1)} %bitcast.42), channel_id=1, source_target_pairs={{0,4},{4,8},{8,12},{12,16},{16,20},{20,24},{24,28},{1,5},{5,9},{9,... | collective-permute-start | bytes 4718600 | tf_op jit(solution)/shard_map/ppermute | solution.py:16
  63.9 7.9 %collective-permute-done.1 = bf16[640,1024]{1,0:T(8,128)(2,1)} collective-permute-done((bf16[640,1024]{1,0:T(8,128)(2,1)}, bf16[640,1024]{1,0:T(8,128)(2,1)}, u32[]{:S(2)}, u32[]{:S(2)}) %collective-permute-start.1) | collective-permute-done | bytes 1310752 | tf_op jit(solution)/shard_map/ppermute | solution.py:16
  71.8 54.7 %collective-permute-done = bf16[768,1024]{1,0:T(8,128)(2,1)} collective-permute-done((bf16[768,1024]{1,0:T(8,128)(2,1)S(1)}, bf16[768,1024]{1,0:T(8,128)(2,1)}, u32[]{:S(2)}, u32[]{:S(2)}) %collective-permute-start) | collective-permute-done | bytes 1572896 | tf_op jit(solution)/shard_map/ppermute | solution.py:16
  126.5 3.6 %pad_maximum_fusion = bf16[2176,1024]{1,0:T(8,128)(2,1)} fusion(bf16[640,1024]{1,0:T(8,128)(2,1)} %collective-permute-done.1, bf16[768,1024]{1,0:T(8,128)(2,1)S(1)} %bitcast.46, bf16[768,1024]{1,0:T(8,128)(2,1)} %collective-permute-done), kind=kLoop, calls=%fused_computation.33 | loop fusion | flops 13369344 | bytes 8912896 | tf_op jit(solution)/shard_map/concatenate | solution.py:75
  130.1 4.2 %fusion.138 = (f32[768]{0:T(1024)S(1)}, f32[768,2176]{0,1:T(8,128)S(1)}) fusion(bf16[768,1024]{1,0:T(8,128)(2,1)} %bitcast.4, bf16[2176,1024]{1,0:T(8,128)(2,1)} %pad_maximum_fusion, pred[2176]{0:T(1024)(128)(4,1)S(1)} %fusion.137, pred[768]{0:T(1024)(128)(4,1)S(1)} %dynamic-slice_compare_fusion, s32[768]{0:T(1024)S(1)} %iota_add_fusion.1, ...), kind=kOutput, calls=%fused_computation.114 | convolution fusion | flops 441187584 | bytes 7467904 | tf_op jit(solution)/shard_map/dot_general | solution.py:39
  134.4 6.3 %fusion.139 = (f32[768]{0:T(1024)S(1)}, f32[768,2176]{0,1:T(8,128)}) fusion(bf16[768,1024]{1,0:T(8,128)(2,1)} %bitcast.4, bf16[2176,1024]{1,0:T(8,128)(2,1)S(1)} %copy-done.1, pred[2176]{0:T(1024)(128)(4,1)S(1)} %fusion.137, pred[768]{0:T(1024)(128)(4,1)S(1)} %dynamic-slice_compare_fusion, s32[768]{0:T(1024)S(1)} %iota_add_fusion.1, ...), kind=kOutput, calls=%fused_computation.115 | convolution fusion | flops 441187584 | bytes 7478272 | tf_op jit(solution)/shard_map/dot_general | solution.py:39
  140.7 5.9 %fusion.140 = (f32[768]{0:T(1024)S(1)}, f32[768,2176]{0,1:T(8,128)}) fusion(bf16[768,1024]{1,0:T(8,128)(2,1)} %bitcast.4, bf16[2176,1024]{1,0:T(8,128)(2,1)S(1)} %copy-done.1, pred[2176]{0:T(1024)(128)(4,1)S(1)} %fusion.137, pred[768]{0:T(1024)(128)(4,1)S(1)} %dynamic-slice_compare_fusion, s32[768]{0:T(1024)S(1)} %iota_add_fusion.1, ...), kind=kOutput, calls=%fused_computation.116 | convolution fusion | flops 441187584 | bytes 7478272 | tf_op jit(solution)/shard_map/dot_general | solution.py:39
  146.6 6.0 %fusion.141 = (f32[768]{0:T(1024)S(1)}, f32[768,2176]{0,1:T(8,128)}) fusion(bf16[768,1024]{1,0:T(8,128)(2,1)} %bitcast.4, bf16[2176,1024]{1,0:T(8,128)(2,1)S(1)} %copy-done.1, pred[2176]{0:T(1024)(128)(4,1)S(1)} %fusion.137, pred[768]{0:T(1024)(128)(4,1)S(1)} %dynamic-slice_compare_fusion, s32[768]{0:T(1024)S(1)} %iota_add_fusion.1, ...), kind=kOutput, calls=%fused_computation.117 | convolution fusion | flops 441187584 | bytes 7478272 | tf_op jit(solution)/shard_map/dot_general | solution.py:39
  152.5 3.6 %fusion.142 = (f32[768]{0:T(1024)S(1)}, f32[768,2176]{0,1:T(8,128)S(1)}) fusion(bf16[768,1024]{1,0:T(8,128)(2,1)} %bitcast.4, bf16[2176,1024]{1,0:T(8,128)(2,1)S(1)} %copy-done.1, pred[2176]{0:T(1024)(128)(4,1)S(1)} %fusion.137, pred[768]{0:T(1024)(128)(4,1)S(1)} %dynamic-slice_compare_fusion, s32[768]{0:T(1024)S(1)} %iota_add_fusion.1, ...), kind=kOutput, calls=%fused_computation.118 | convolution fusion | flops 441187584 | bytes 7478272 | tf_op jit(solution)/shard_map/dot_general | solution.py:39
  156.2 3.6 %fusion.143 = (f32[768]{0:T(1024)S(1)}, f32[768,2176]{0,1:T(8,128)S(1)}) fusion(bf16[768,1024]{1,0:T(8,128)(2,1)} %bitcast.4, bf16[2176,1024]{1,0:T(8,128)(2,1)S(1)} %copy-done.1, pred[2176]{0:T(1024)(128)(4,1)S(1)} %fusion.137, pred[768]{0:T(1024)(128)(4,1)S(1)} %dynamic-slice_compare_fusion, s32[768]{0:T(1024)S(1)} %iota_add_fusion.1, ...), kind=kOutput, calls=%fused_computation.119 | convolution fusion | flops 441187584 | bytes 7478272 | tf_op jit(solution)/shard_map/dot_general | solution.py:39
  160.8 3.6 %fusion.144 = (f32[768]{0:T(1024)S(1)}, f32[768,2176]{0,1:T(8,128)S(1)}) fusion(bf16[768,1024]{1,0:T(8,128)(2,1)} %bitcast.4, bf16[2176,1024]{1,0:T(8,128)(2,1)S(1)} %copy-done.1, pred[2176]{0:T(1024)(128)(4,1)S(1)} %fusion.137, pred[768]{0:T(1024)(128)(4,1)S(1)} %dynamic-slice_compare_fusion, s32[768]{0:T(1024)S(1)} %iota_add_fusion.1, ...), kind=kOutput, calls=%fused_computation.120 | convolution fusion | flops 441187584 | bytes 7478272 | tf_op jit(solution)/shard_map/dot_general | solution.py:39
  164.5 3.9 %fusion.145 = (f32[768]{0:T(1024)S(1)}, f32[768,2176]{0,1:T(8,128)S(1)}) fusion(bf16[768,1024]{1,0:T(8,128)(2,1)} %bitcast.4, bf16[2176,1024]{1,0:T(8,128)(2,1)S(1)} %copy-done.1, pred[2176]{0:T(1024)(128)(4,1)S(1)} %fusion.137, pred[768]{0:T(1024)(128)(4,1)S(1)} %dynamic-slice_compare_fusion, s32[768]{0:T(1024)S(1)} %iota_add_fusion.1, ...), kind=kOutput, calls=%fused_computation.121 | convolution fusion | flops 441187584 | bytes 7478272 | tf_op jit(solution)/shard_map/dot_general | solution.py:39
  168.4 3.9 %pad_maximum_fusion.1 = bf16[2176,1024]{1,0:T(8,128)(2,1)} fusion(bf16[640,1024]{1,0:T(8,128)(2,1)} %collective-permute-done.3, bf16[768,1024]{1,0:T(8,128)(2,1)S(1)} %bitcast.43, bf16[768,1024]{1,0:T(8,128)(2,1)} %collective-permute-done.2), kind=kLoop, calls=%fused_computation.34 | loop fusion | flops 13369344 | bytes 8912896 | tf_op jit(solution)/shard_map/concatenate | solution.py:78
  172.2 4.3 %fusion.46 = bf16[768,1024]{0,1:T(8,128)(2,1)S(1)} fusion(f32[768,2176]{0,1:T(8,128)} %copy-done, f32[768]{0:T(1024)S(1)} %get-tuple-element.7, bf16[2176,1024]{1,0:T(8,128)(2,1)} %pad_maximum_fusion.1, f32[768]{0:T(1024)S(1)} %fusion), kind=kOutput, calls=%fused_computation.56 | convolution fusion | flops 431357952 | bytes 7444480 | tf_op jit(solution)/shard_map/dot_general | solution.py:49
  179.8 4.0 %fusion.4 = f32[768]{0:T(1024)S(1)} fusion(f32[768,2176]{0,1:T(8,128)} %get-tuple-element.12, f32[768]{0:T(1024)S(1)} %get-tuple-element.11), kind=kLoop, calls=%fused_computation.21 | loop fusion | flops 3341568 | bytes 6690816 | tf_op jit(solution)/shard_map/reduce_sum | solution.py:47
  183.8 4.3 %fusion.64 = bf16[768,1024]{0,1:T(8,128)(2,1)S(1)} fusion(bf16[768,1024]{0,1:T(8,128)(2,1)S(1)} %fusion.55, f32[768,2176]{0,1:T(8,128)} %get-tuple-element.12, f32[768]{0:T(1024)S(1)} %get-tuple-element.11, bf16[2176,1024]{1,0:T(8,128)(2,1)} %pad_maximum_fusion.1, f32[768]{0:T(1024)S(1)} %fusion.4), kind=kOutput, calls=%fused_computation.62 | convolution fusion | flops 431357952 | bytes 7446528 | tf_op jit(solution)/shard_map/dot_general | solution.py:49
  206.2 3.6 %all-to-all-start.3 = ((bf16[4,192,1024]{2,1,0:T(8,128)(2,1)}), bf16[4,192,1024]{2,1,0:T(8,128)(2,1)S(1)}, u32[]{:S(2)}, u32[]{:S(2)}) async-start(bf16[4,192,1024]{2,1,0:T(8,128)(2,1)} %bitcast.17), calls=%async_computation.3 | async-start | bytes 3145728 | tf_op jit(solution)/shard_map/all_to_all | solution.py:100
  210.0 60.4 %all-reduce.2 = (f32[16]{0:T(128)S(1)}, f32[16]{0:T(128)S(1)}) all-reduce(f32[16]{0:T(128)S(1)} %get-tuple-element.4, f32[16]{0:T(128)S(1)} %get-tuple-element.3), channel_id=1, replica_groups=mesh['seq'=8,'head'=4] {'seq','head'}, use_global_device_ids=true, to_apply=%region_17.18 | all-reduce | flops 32 | bytes 256 | tf_op jit(solution)/shard_map/psum | solution.py:112
  (62 shorter events, 36.3 us)
Async XLA Ops:
  0.6 7.1 %copy-start.2 = (bf16[192,4096]{1,0:T(8,128)(2,1)S(1)}, bf16[192,4096]{1,0:T(8,128)(2,1)}, u32[]{:S(2)}) copy-start(bf16[192,4096]{1,0:T(8,128)(2,1)} %param.9) | copy-start | bytes 4718596
  3.5 24.3 %all-to-all-start = ((bf16[192,4,1024]{2,0,1:T(8,128)(2,1)}), bf16[192,4,1024]{2,0,1:T(8,128)(2,1)S(1)}, u32[]{:S(2)}, u32[]{:S(2)}) async-start(bf16[192,4,1024]{2,0,1:T(8,128)(2,1)} %bitcast.40), calls=%async_computation | async-start | bytes 3145728 | tf_op jit(solution)/shard_map/all_to_all | solution.py:59
  27.7 23.6 %all-to-all-start.2 = ((bf16[192,4,1024]{2,0,1:T(8,128)(2,1)}), bf16[192,4,1024]{2,0,1:T(8,128)(2,1)S(1)}, u32[]{:S(2)}, u32[]{:S(2)}) async-start(bf16[192,4,1024]{2,0,1:T(8,128)(2,1)} %bitcast.53), calls=%async_computation.2 | async-start | bytes 3145728 | tf_op jit(solution)/shard_map/all_to_all | solution.py:60
  31.3 24.4 %copy-start.3 = (s32[6144]{0:T(1024)S(1)}, s32[6144]{0:T(1024)}, u32[]{:S(2)}) copy-start(s32[6144]{0:T(1024)} %param.10) | copy-start | bytes 73732
  31.3 24.5 %copy-start.4 = (s32[6144]{0:T(1024)S(1)}, s32[6144]{0:T(1024)}, u32[]{:S(2)}) copy-start(s32[6144]{0:T(1024)} %param.11) | copy-start | bytes 73732
  31.3 95.2 %collective-permute-start = (bf16[768,1024]{1,0:T(8,128)(2,1)S(1)}, bf16[768,1024]{1,0:T(8,128)(2,1)}, u32[]{:S(2)}, u32[]{:S(2)}) collective-permute-start(bf16[768,1024]{1,0:T(8,128)(2,1)S(1)} %bitcast.44), channel_id=1, source_target_pairs={{0,4},{4,8},{8,12},{12,16},{16,20},{20,24},{24,28},{1,5},{5,9},{9,... | collective-permute-start | bytes 4718600 | tf_op jit(solution)/shard_map/ppermute | solution.py:16
  37.9 33.8 %collective-permute-start.1 = (bf16[640,1024]{1,0:T(8,128)(2,1)}, bf16[640,1024]{1,0:T(8,128)(2,1)}, u32[]{:S(2)}, u32[]{:S(2)}) collective-permute-start(bf16[640,1024]{1,0:T(8,128)(2,1)} %slice.104), channel_id=1, source_target_pairs={{4,0},{8,4},{12,8},{16,12},{20,16},{24,20},{28,24},{5,1},{9,5},{13... | collective-permute-start | bytes 3932168 | tf_op jit(solution)/shard_map/ppermute | solution.py:16
  51.3 78.8 %all-to-all-start.1 = ((bf16[192,4,1024]{2,0,1:T(8,128)(2,1)}), bf16[192,4,1024]{2,0,1:T(8,128)(2,1)}, u32[]{:S(2)}, u32[]{:S(2)}) async-start(bf16[192,4,1024]{2,0,1:T(8,128)(2,1)} %bitcast.51), calls=%async_computation.1 | async-start | bytes 3145728 | tf_op jit(solution)/shard_map/all_to_all | solution.py:58
  57.2 111.1 %collective-permute-start.2 = (bf16[768,1024]{1,0:T(8,128)(2,1)S(1)}, bf16[768,1024]{1,0:T(8,128)(2,1)}, u32[]{:S(2)}, u32[]{:S(2)}) collective-permute-start(bf16[768,1024]{1,0:T(8,128)(2,1)S(1)} %bitcast.42), channel_id=1, source_target_pairs={{0,4},{4,8},{8,12},{12,16},{16,20},{20,24},{24,28},{1,5},{5,9},{9,... | collective-permute-start | bytes 4718600 | tf_op jit(solution)/shard_map/ppermute | solution.py:16
  62.6 105.8 %collective-permute-start.3 = (bf16[640,1024]{1,0:T(8,128)(2,1)}, bf16[640,1024]{1,0:T(8,128)(2,1)}, u32[]{:S(2)}, u32[]{:S(2)}) collective-permute-start(bf16[640,1024]{1,0:T(8,128)(2,1)} %slice.107), channel_id=1, source_target_pairs={{4,0},{8,4},{12,8},{16,12},{20,16},{24,20},{28,24},{5,1},{9,5},{13... | collective-permute-start | bytes 3932168 | tf_op jit(solution)/shard_map/ppermute | solution.py:16
  130.1 4.2 %copy-start.1 = (bf16[2176,1024]{1,0:T(8,128)(2,1)S(1)}, bf16[2176,1024]{1,0:T(8,128)(2,1)}, u32[]{:S(2)}) copy-start(bf16[2176,1024]{1,0:T(8,128)(2,1)} %pad_maximum_fusion) | copy-start | bytes 13369348
  134.4 25.5 %copy-start = (f32[768,2176]{0,1:T(8,128)}, f32[768,2176]{0,1:T(8,128)S(1)}, u32[]{:S(2)}) copy-start(f32[768,2176]{0,1:T(8,128)S(1)} %get-tuple-element.8) | copy-start | bytes 20054020
  168.3 8.2 %slice-start.2 = ((s8[6684672]{0:T(1024)(128)(4,1)}), s8[4194304]{0:T(1024)(128)(4,1)S(1)}, s32[]{:S(2)}) async-start(s8[6684672]{0:T(1024)(128)(4,1)} %bitcast.49), calls=%async_computation.6 | async-start | bytes 8388608
  172.2 4.3 %slice-start.3 = ((s8[6684672]{0:T(1024)(128)(4,1)}), s8[2490368]{0:T(1024)(128)(4,1)S(1)}, s32[]{:S(2)}) async-start(s8[6684672]{0:T(1024)(128)(4,1)} %bitcast.49), calls=%async_computation.7 | async-start | bytes 4980736
  179.8 8.3 %slice-start = ((s8[6684672]{0:T(1024)(128)(4,1)}), s8[4194304]{0:T(1024)(128)(4,1)S(1)}, s32[]{:S(2)}) async-start(s8[6684672]{0:T(1024)(128)(4,1)} %bitcast.47), calls=%async_computation.4 | async-start | bytes 8388608
  183.8 4.3 %slice-start.1 = ((s8[6684672]{0:T(1024)(128)(4,1)}), s8[2490368]{0:T(1024)(128)(4,1)S(1)}, s32[]{:S(2)}) async-start(s8[6684672]{0:T(1024)(128)(4,1)} %bitcast.47), calls=%async_computation.5 | async-start | bytes 4980736
  204.5 5.3 %copy-start.6 = (s32[192]{0:T(256)S(1)}, s32[192]{0:T(256)}, u32[]{:S(2)}) copy-start(s32[192]{0:T(256)} %param.12) | copy-start | bytes 2308
  204.5 5.3 %copy-start.5 = (f32[192]{0:T(256)S(1)}, f32[192]{0:T(256)}, u32[]{:S(2)}) copy-start(f32[192]{0:T(256)} %param.13) | copy-start | bytes 2308
  206.2 64.7 %all-to-all-start.3 = ((bf16[4,192,1024]{2,1,0:T(8,128)(2,1)}), bf16[4,192,1024]{2,1,0:T(8,128)(2,1)S(1)}, u32[]{:S(2)}, u32[]{:S(2)}) async-start(bf16[4,192,1024]{2,1,0:T(8,128)(2,1)} %bitcast.17), calls=%async_computation.3 | async-start | bytes 3145728 | tf_op jit(solution)/shard_map/all_to_all | solution.py:100
  270.3 1.8 copy-start.7
where the time goes:
time: 273 us; the launch traced here: 272 us
  waiting for transfers between devices  90.8 us (33%)
  blocking collectives  60.4 us (22%)
  matrix products  59.3 us (22%)
  starting transfers between devices  29 us (11%)
  other arithmetic  19.2 us (7%)
  local copies, waits for them, and re-layouts  12.4 us (5%)
    ppermute x4, waiting for transfers between devices, shifted(): return lax.ppermute(block, axis, route)  62.6 us
    psum x1, blocking collectives, per_device(): counts, sums = lax.psum((counts, sums), ('seq', 'head'))  60.4 us
    dot_general x8, matrix products, attend(): lax.dot_general(query_head, key_head, (((1,), (1,)), ((), ())), preferred...  37.1 us
    dot_general x8, matrix products, attend(): jnp.dot(weights.astype(jnp.bfloat16), value_head, preferred_element_type=...  22.2 us
    all_to_all x1, waiting for transfers between devices, per_device(): lax.all_to_all(key_rows, 'head', split_axis=1, concat_axis=0, tiled=True)  18.7 us
    ppermute x4, starting transfers between devices, shifted(): return lax.ppermute(block, axis, route)  13.3 us
    reduce_sum x8, other arithmetic, attend(): total = jnp.sum(weights, axis=1, keepdims=True)  10.9 us
    all_to_all x1, waiting for transfers between devices, per_device(): lax.all_to_all(values, 'head', split_axis=1, concat_axis=0, tiled=True)  9.44 us
  transfers between devices with their start and end apart: 8, of which 4 were waited for; matrix products, arithmetic and copies ran while one was open for 18% of the time, Pallas kernels for 0%

commit v1 on v0

--- a/solution.py
+++ b/solution.py
@@ -56,7 +56,12 @@
 def per_device(queries, key_rows, values, doc_ids, image_flags, labels, token_loss):
     query_local, key_local, value_local = (
         lax.all_to_all(queries, "head", split_axis=1, concat_axis=0, tiled=True),
-        lax.all_to_all(key_rows, "head", split_axis=1, concat_axis=0, tiled=True),
+        jnp.concatenate(
+            lax.all_to_all(
+                jnp.stack(jnp.split(key_rows, lax.axis_size("head"), axis=1)), "head", 0, 0
+            ),
+            axis=0,
+        ),
         lax.all_to_all(values, "head", split_axis=1, concat_axis=0, tiled=True),
     )
     reach_back = (DOC_MOST + TOK_DEV - 2) // TOK_DEV

time: 273 us -> 273 us (level)
    all_to_all x1 -> x0, local copies, waits for them, and re-layouts: 2.82 us -> none  [per_device(): lax.all_to_all(key_rows, 'head', split_axis=1, concat_axis=0, tiled=True)]
where the time goes in v1:
time: 273 us; the launch traced here: 272 us
  waiting for transfers between devices  90.8 us (33%)
  blocking collectives  60.4 us (22%)
  matrix products  59.3 us (22%)
  starting transfers between devices  29 us (11%)
  other arithmetic  20.6 us (8%)
  local copies, waits for them, and re-layouts  11.2 us (4%)
    ppermute x4, waiting for transfers between devices, shifted(): return lax.ppermute(block, axis, route)  62.6 us
    psum x1, blocking collectives, per_device(): counts, sums = lax.psum((counts, sums), ('seq', 'head'))  60.4 us
    dot_general x8, matrix products, attend(): lax.dot_general(query_head, key_head, (((1,), (1,)), ((), ())), preferred...  37.2 us
    dot_general x8, matrix products, attend(): jnp.dot(weights.astype(jnp.bfloat16), value_head, preferred_element_type=...  22.2 us
    all_to_all x1, waiting for transfers between devices, per_device(): lax.all_to_all(jnp.stack(jnp.split(key_rows, lax.axis_size('head'), axis=...  18.7 us
    ppermute x4, starting transfers between devices, shifted(): return lax.ppermute(block, axis, route)  13.3 us
    reduce_sum x8, other arithmetic, attend(): total = jnp.sum(weights, axis=1, keepdims=True)  10.9 us
    all_to_all x1, waiting for transfers between devices, per_device(): lax.all_to_all(values, 'head', split_axis=1, concat_axis=0, tiled=True)  9.44 us
  transfers between devices with their start and end apart: 8, of which 4 were waited for; matrix products, arithmetic and copies ran while one was open for 18% of the time, Pallas kernels for 0%

profile of v1, /device:TPU:0, one launch (start us, length us, event | category | flops | bytes accessed | tf_op | source)
XLA Modules:
  0.0 272.3 jit_solution(2636868037146751547)
XLA Ops:
  3.6 4.2 %all-to-all-start = ((bf16[4,192,1024]{2,1,0:T(8,128)(2,1)}), bf16[4,192,1024]{2,1,0:T(8,128)(2,1)S(1)}, u32[]{:S(2)}, u32[]{:S(2)}) async-start(bf16[4,192,1024]{2,1,0:T(8,128)(2,1)} %pad_maximum_fusion.2), calls=%async_computation | async-start | bytes 3145728 | tf_op jit(solution)/shard_map/all_to_all | solution.py:60
  9.2 18.7 %all-to-all-done = bf16[4,192,1024]{2,1,0:T(8,128)(2,1)S(1)} async-done(((bf16[4,192,1024]{2,1,0:T(8,128)(2,1)}), bf16[4,192,1024]{2,1,0:T(8,128)(2,1)S(1)}, u32[]{:S(2)}, u32[]{:S(2)}) %all-to-all-start) | async-done | bytes 1572896 | tf_op jit(solution)/shard_map/all_to_all | solution.py:60
  27.9 3.6 %all-to-all-start.2 = ((bf16[192,4,1024]{2,0,1:T(8,128)(2,1)}), bf16[192,4,1024]{2,0,1:T(8,128)(2,1)S(1)}, u32[]{:S(2)}, u32[]{:S(2)}) async-start(bf16[192,4,1024]{2,0,1:T(8,128)(2,1)} %bitcast.55), calls=%async_computation.2 | async-start | bytes 3145728 | tf_op jit(solution)/shard_map/all_to_all | solution.py:65
  31.5 5.4 %collective-permute-start = (bf16[768,1024]{1,0:T(8,128)(2,1)S(1)}, bf16[768,1024]{1,0:T(8,128)(2,1)}, u32[]{:S(2)}, u32[]{:S(2)}) collective-permute-start(bf16[768,1024]{1,0:T(8,128)(2,1)S(1)} %bitcast.46), channel_id=1, source_target_pairs={{0,4},{4,8},{8,12},{12,16},{16,20},{20,24},{24,28},{1,5},{5,9},{9,... | collective-permute-start | bytes 4718600 | tf_op jit(solution)/shard_map/ppermute | solution.py:16
  42.0 9.4 %all-to-all-done.2 = bf16[192,4,1024]{2,0,1:T(8,128)(2,1)S(1)} async-done(((bf16[192,4,1024]{2,0,1:T(8,128)(2,1)}), bf16[192,4,1024]{2,0,1:T(8,128)(2,1)S(1)}, u32[]{:S(2)}, u32[]{:S(2)}) %all-to-all-start.2) | async-done | bytes 1572896 | tf_op jit(solution)/shard_map/all_to_all | solution.py:65
  51.5 4.3 %all-to-all-start.1 = ((bf16[192,4,1024]{2,0,1:T(8,128)(2,1)}), bf16[192,4,1024]{2,0,1:T(8,128)(2,1)}, u32[]{:S(2)}, u32[]{:S(2)}) async-start(bf16[192,4,1024]{2,0,1:T(8,128)(2,1)} %bitcast.53), calls=%async_computation.1 | async-start | bytes 3145728 | tf_op jit(solution)/shard_map/all_to_all | solution.py:58
  57.4 5.3 %collective-permute-start.2 = (bf16[768,1024]{1,0:T(8,128)(2,1)S(1)}, bf16[768,1024]{1,0:T(8,128)(2,1)}, u32[]{:S(2)}, u32[]{:S(2)}) collective-permute-start(bf16[768,1024]{1,0:T(8,128)(2,1)S(1)} %bitcast.44), channel_id=1, source_target_pairs={{0,4},{4,8},{8,12},{12,16},{16,20},{20,24},{24,28},{1,5},{5,9},{9,... | collective-permute-start | bytes 4718600 | tf_op jit(solution)/shard_map/ppermute | solution.py:16
  64.0 7.9 %collective-permute-done.1 = bf16[640,1024]{1,0:T(8,128)(2,1)} collective-permute-done((bf16[640,1024]{1,0:T(8,128)(2,1)}, bf16[640,1024]{1,0:T(8,128)(2,1)}, u32[]{:S(2)}, u32[]{:S(2)}) %collective-permute-start.1) | collective-permute-done | bytes 1310752 | tf_op jit(solution)/shard_map/ppermute | solution.py:16
  71.9 54.7 %collective-permute-done = bf16[768,1024]{1,0:T(8,128)(2,1)} collective-permute-done((bf16[768,1024]{1,0:T(8,128)(2,1)S(1)}, bf16[768,1024]{1,0:T(8,128)(2,1)}, u32[]{:S(2)}, u32[]{:S(2)}) %collective-permute-start) | collective-permute-done | bytes 1572896 | tf_op jit(solution)/shard_map/ppermute | solution.py:16
  126.6 3.6 %pad_maximum_fusion = bf16[2176,1024]{1,0:T(8,128)(2,1)} fusion(bf16[640,1024]{1,0:T(8,128)(2,1)} %collective-permute-done.1, bf16[768,1024]{1,0:T(8,128)(2,1)S(1)} %bitcast.48, bf16[768,1024]{1,0:T(8,128)(2,1)} %collective-permute-done), kind=kLoop, calls=%fused_computation.33 | loop fusion | flops 13369344 | bytes 8912896 | tf_op jit(solution)/shard_map/concatenate | solution.py:80
  130.3 4.2 %fusion.138 = (f32[768]{0:T(1024)S(1)}, f32[768,2176]{0,1:T(8,128)S(1)}) fusion(bf16[768,1024]{1,0:T(8,128)(2,1)} %bitcast.6, bf16[2176,1024]{1,0:T(8,128)(2,1)} %pad_maximum_fusion, pred[2176]{0:T(1024)(128)(4,1)S(1)} %fusion.137, pred[768]{0:T(1024)(128)(4,1)S(1)} %dynamic-slice_compare_fusion, s32[768]{0:T(1024)S(1)} %iota_add_fusion.1, ...), kind=kOutput, calls=%fused_computation.118 | convolution fusion | flops 441187584 | bytes 7467904 | tf_op jit(solution)/shard_map/dot_general | solution.py:39
  134.6 6.3 %fusion.139 = (f32[768]{0:T(1024)S(1)}, f32[768,2176]{0,1:T(8,128)}) fusion(bf16[768,1024]{1,0:T(8,128)(2,1)} %bitcast.6, bf16[2176,1024]{1,0:T(8,128)(2,1)S(1)} %copy-done.1, pred[2176]{0:T(1024)(128)(4,1)S(1)} %fusion.137, pred[768]{0:T(1024)(128)(4,1)S(1)} %dynamic-slice_compare_fusion, s32[768]{0:T(1024)S(1)} %iota_add_fusion.1, ...), kind=kOutput, calls=%fused_computation.119 | convolution fusion | flops 441187584 | bytes 7478272 | tf_op jit(solution)/shard_map/dot_general | solution.py:39
  140.8 5.9 %fusion.140 = (f32[768]{0:T(1024)S(1)}, f32[768,2176]{0,1:T(8,128)}) fusion(bf16[768,1024]{1,0:T(8,128)(2,1)} %bitcast.6, bf16[2176,1024]{1,0:T(8,128)(2,1)S(1)} %copy-done.1, pred[2176]{0:T(1024)(128)(4,1)S(1)} %fusion.137, pred[768]{0:T(1024)(128)(4,1)S(1)} %dynamic-slice_compare_fusion, s32[768]{0:T(1024)S(1)} %iota_add_fusion.1, ...), kind=kOutput, calls=%fused_computation.120 | convolution fusion | flops 441187584 | bytes 7478272 | tf_op jit(solution)/shard_map/dot_general | solution.py:39
  146.7 6.0 %fusion.141 = (f32[768]{0:T(1024)S(1)}, f32[768,2176]{0,1:T(8,128)}) fusion(bf16[768,1024]{1,0:T(8,128)(2,1)} %bitcast.6, bf16[2176,1024]{1,0:T(8,128)(2,1)S(1)} %copy-done.1, pred[2176]{0:T(1024)(128)(4,1)S(1)} %fusion.137, pred[768]{0:T(1024)(128)(4,1)S(1)} %dynamic-slice_compare_fusion, s32[768]{0:T(1024)S(1)} %iota_add_fusion.1, ...), kind=kOutput, calls=%fused_computation.121 | convolution fusion | flops 441187584 | bytes 7478272 | tf_op jit(solution)/shard_map/dot_general | solution.py:39
  152.7 3.6 %fusion.142 = (f32[768]{0:T(1024)S(1)}, f32[768,2176]{0,1:T(8,128)S(1)}) fusion(bf16[768,1024]{1,0:T(8,128)(2,1)} %bitcast.6, bf16[2176,1024]{1,0:T(8,128)(2,1)S(1)} %copy-done.1, pred[2176]{0:T(1024)(128)(4,1)S(1)} %fusion.137, pred[768]{0:T(1024)(128)(4,1)S(1)} %dynamic-slice_compare_fusion, s32[768]{0:T(1024)S(1)} %iota_add_fusion.1, ...), kind=kOutput, calls=%fused_computation.122 | convolution fusion | flops 441187584 | bytes 7478272 | tf_op jit(solution)/shard_map/dot_general | solution.py:39
  156.3 3.6 %fusion.143 = (f32[768]{0:T(1024)S(1)}, f32[768,2176]{0,1:T(8,128)S(1)}) fusion(bf16[768,1024]{1,0:T(8,128)(2,1)} %bitcast.6, bf16[2176,1024]{1,0:T(8,128)(2,1)S(1)} %copy-done.1, pred[2176]{0:T(1024)(128)(4,1)S(1)} %fusion.137, pred[768]{0:T(1024)(128)(4,1)S(1)} %dynamic-slice_compare_fusion, s32[768]{0:T(1024)S(1)} %iota_add_fusion.1, ...), kind=kOutput, calls=%fused_computation.123 | convolution fusion | flops 441187584 | bytes 7478272 | tf_op jit(solution)/shard_map/dot_general | solution.py:39
  161.0 3.6 %fusion.144 = (f32[768]{0:T(1024)S(1)}, f32[768,2176]{0,1:T(8,128)S(1)}) fusion(bf16[768,1024]{1,0:T(8,128)(2,1)} %bitcast.6, bf16[2176,1024]{1,0:T(8,128)(2,1)S(1)} %copy-done.1, pred[2176]{0:T(1024)(128)(4,1)S(1)} %fusion.137, pred[768]{0:T(1024)(128)(4,1)S(1)} %dynamic-slice_compare_fusion, s32[768]{0:T(1024)S(1)} %iota_add_fusion.1, ...), kind=kOutput, calls=%fused_computation.124 | convolution fusion | flops 441187584 | bytes 7478272 | tf_op jit(solution)/shard_map/dot_general | solution.py:39
  164.6 3.9 %fusion.145 = (f32[768]{0:T(1024)S(1)}, f32[768,2176]{0,1:T(8,128)S(1)}) fusion(bf16[768,1024]{1,0:T(8,128)(2,1)} %bitcast.6, bf16[2176,1024]{1,0:T(8,128)(2,1)S(1)} %copy-done.1, pred[2176]{0:T(1024)(128)(4,1)S(1)} %fusion.137, pred[768]{0:T(1024)(128)(4,1)S(1)} %dynamic-slice_compare_fusion, s32[768]{0:T(1024)S(1)} %iota_add_fusion.1, ...), kind=kOutput, calls=%fused_computation.125 | convolution fusion | flops 441187584 | bytes 7478272 | tf_op jit(solution)/shard_map/dot_general | solution.py:39
  168.5 3.9 %pad_maximum_fusion.1 = bf16[2176,1024]{1,0:T(8,128)(2,1)} fusion(bf16[640,1024]{1,0:T(8,128)(2,1)} %collective-permute-done.3, bf16[768,1024]{1,0:T(8,128)(2,1)S(1)} %bitcast.45, bf16[768,1024]{1,0:T(8,128)(2,1)} %collective-permute-done.2), kind=kLoop, calls=%fused_computation.34 | loop fusion | flops 13369344 | bytes 8912896 | tf_op jit(solution)/shard_map/concatenate | solution.py:83
  172.4 4.3 %fusion.46 = bf16[768,1024]{0,1:T(8,128)(2,1)S(1)} fusion(f32[768,2176]{0,1:T(8,128)} %copy-done, f32[768]{0:T(1024)S(1)} %get-tuple-element.11, bf16[2176,1024]{1,0:T(8,128)(2,1)} %pad_maximum_fusion.1, f32[768]{0:T(1024)S(1)} %fusion), kind=kOutput, calls=%fused_computation.56 | convolution fusion | flops 431357952 | bytes 7444480 | tf_op jit(solution)/shard_map/dot_general | solution.py:49
  180.0 4.0 %fusion.4 = f32[768]{0:T(1024)S(1)} fusion(f32[768,2176]{0,1:T(8,128)} %get-tuple-element.16, f32[768]{0:T(1024)S(1)} %get-tuple-element.15), kind=kLoop, calls=%fused_computation.21 | loop fusion | flops 3341568 | bytes 6690816 | tf_op jit(solution)/shard_map/reduce_sum | solution.py:47
  184.0 4.3 %fusion.64 = bf16[768,1024]{0,1:T(8,128)(2,1)S(1)} fusion(bf16[768,1024]{0,1:T(8,128)(2,1)S(1)} %fusion.55, f32[768,2176]{0,1:T(8,128)} %get-tuple-element.16, f32[768]{0:T(1024)S(1)} %get-tuple-element.15, bf16[2176,1024]{1,0:T(8,128)(2,1)} %pad_maximum_fusion.1, f32[768]{0:T(1024)S(1)} %fusion.4), kind=kOutput, calls=%fused_computation.62 | convolution fusion | flops 431357952 | bytes 7446528 | tf_op jit(solution)/shard_map/dot_general | solution.py:49
  206.3 3.6 %all-to-all-start.3 = ((bf16[4,192,1024]{2,1,0:T(8,128)(2,1)}), bf16[4,192,1024]{2,1,0:T(8,128)(2,1)S(1)}, u32[]{:S(2)}, u32[]{:S(2)}) async-start(bf16[4,192,1024]{2,1,0:T(8,128)(2,1)} %bitcast.19), calls=%async_computation.3 | async-start | bytes 3145728 | tf_op jit(solution)/shard_map/all_to_all | solution.py:105
  210.1 60.4 %all-reduce.2 = (f32[16]{0:T(128)S(1)}, f32[16]{0:T(128)S(1)}) all-reduce(f32[16]{0:T(128)S(1)} %get-tuple-element.4, f32[16]{0:T(128)S(1)} %get-tuple-element.3), channel_id=1, replica_groups=mesh['seq'=8,'head'=4] {'seq','head'}, use_global_device_ids=true, to_apply=%region_17.18 | all-reduce | flops 32 | bytes 256 | tf_op jit(solution)/shard_map/psum | solution.py:117
  (63 shorter events, 36.4 us)
Async XLA Ops:
  0.6 7.2 %copy-start.2 = (bf16[192,4096]{1,0:T(8,128)(2,1)S(1)}, bf16[192,4096]{1,0:T(8,128)(2,1)}, u32[]{:S(2)}) copy-start(bf16[192,4096]{1,0:T(8,128)(2,1)} %param.9) | copy-start | bytes 4718596
  3.6 24.3 %all-to-all-start = ((bf16[4,192,1024]{2,1,0:T(8,128)(2,1)}), bf16[4,192,1024]{2,1,0:T(8,128)(2,1)S(1)}, u32[]{:S(2)}, u32[]{:S(2)}) async-start(bf16[4,192,1024]{2,1,0:T(8,128)(2,1)} %pad_maximum_fusion.2), calls=%async_computation | async-start | bytes 3145728 | tf_op jit(solution)/shard_map/all_to_all | solution.py:60
  27.9 23.6 %all-to-all-start.2 = ((bf16[192,4,1024]{2,0,1:T(8,128)(2,1)}), bf16[192,4,1024]{2,0,1:T(8,128)(2,1)S(1)}, u32[]{:S(2)}, u32[]{:S(2)}) async-start(bf16[192,4,1024]{2,0,1:T(8,128)(2,1)} %bitcast.55), calls=%async_computation.2 | async-start | bytes 3145728 | tf_op jit(solution)/shard_map/all_to_all | solution.py:65
  31.5 24.4 %copy-start.3 = (s32[6144]{0:T(1024)S(1)}, s32[6144]{0:T(1024)}, u32[]{:S(2)}) copy-start(s32[6144]{0:T(1024)} %param.10) | copy-start | bytes 73732
  31.5 24.5 %copy-start.4 = (s32[6144]{0:T(1024)S(1)}, s32[6144]{0:T(1024)}, u32[]{:S(2)}) copy-start(s32[6144]{0:T(1024)} %param.11) | copy-start | bytes 73732
  31.5 95.2 %collective-permute-start = (bf16[768,1024]{1,0:T(8,128)(2,1)S(1)}, bf16[768,1024]{1,0:T(8,128)(2,1)}, u32[]{:S(2)}, u32[]{:S(2)}) collective-permute-start(bf16[768,1024]{1,0:T(8,128)(2,1)S(1)} %bitcast.46), channel_id=1, source_target_pairs={{0,4},{4,8},{8,12},{12,16},{16,20},{20,24},{24,28},{1,5},{5,9},{9,... | collective-permute-start | bytes 4718600 | tf_op jit(solution)/shard_map/ppermute | solution.py:16
  38.1 33.8 %collective-permute-start.1 = (bf16[640,1024]{1,0:T(8,128)(2,1)}, bf16[640,1024]{1,0:T(8,128)(2,1)}, u32[]{:S(2)}, u32[]{:S(2)}) collective-permute-start(bf16[640,1024]{1,0:T(8,128)(2,1)} %slice.104), channel_id=1, source_target_pairs={{4,0},{8,4},{12,8},{16,12},{20,16},{24,20},{28,24},{5,1},{9,5},{13... | collective-permute-start | bytes 3932168 | tf_op jit(solution)/shard_map/ppermute | solution.py:16
  51.5 78.8 %all-to-all-start.1 = ((bf16[192,4,1024]{2,0,1:T(8,128)(2,1)}), bf16[192,4,1024]{2,0,1:T(8,128)(2,1)}, u32[]{:S(2)}, u32[]{:S(2)}) async-start(bf16[192,4,1024]{2,0,1:T(8,128)(2,1)} %bitcast.53), calls=%async_computation.1 | async-start | bytes 3145728 | tf_op jit(solution)/shard_map/all_to_all | solution.py:58
  57.4 111.1 %collective-permute-start.2 = (bf16[768,1024]{1,0:T(8,128)(2,1)S(1)}, bf16[768,1024]{1,0:T(8,128)(2,1)}, u32[]{:S(2)}, u32[]{:S(2)}) collective-permute-start(bf16[768,1024]{1,0:T(8,128)(2,1)S(1)} %bitcast.44), channel_id=1, source_target_pairs={{0,4},{4,8},{8,12},{12,16},{16,20},{20,24},{24,28},{1,5},{5,9},{9,... | collective-permute-start | bytes 4718600 | tf_op jit(solution)/shard_map/ppermute | solution.py:16
  62.7 105.8 %collective-permute-start.3 = (bf16[640,1024]{1,0:T(8,128)(2,1)}, bf16[640,1024]{1,0:T(8,128)(2,1)}, u32[]{:S(2)}, u32[]{:S(2)}) collective-permute-start(bf16[640,1024]{1,0:T(8,128)(2,1)} %slice.107), channel_id=1, source_target_pairs={{4,0},{8,4},{12,8},{16,12},{20,16},{24,20},{28,24},{5,1},{9,5},{13... | collective-permute-start | bytes 3932168 | tf_op jit(solution)/shard_map/ppermute | solution.py:16
  130.3 4.2 %copy-start.1 = (bf16[2176,1024]{1,0:T(8,128)(2,1)S(1)}, bf16[2176,1024]{1,0:T(8,128)(2,1)}, u32[]{:S(2)}) copy-start(bf16[2176,1024]{1,0:T(8,128)(2,1)} %pad_maximum_fusion) | copy-start | bytes 13369348
  134.5 25.5 %copy-start = (f32[768,2176]{0,1:T(8,128)}, f32[768,2176]{0,1:T(8,128)S(1)}, u32[]{:S(2)}) copy-start(f32[768,2176]{0,1:T(8,128)S(1)} %get-tuple-element.12) | copy-start | bytes 20054020
  168.5 8.2 %slice-start.2 = ((s8[6684672]{0:T(1024)(128)(4,1)}), s8[4194304]{0:T(1024)(128)(4,1)S(1)}, s32[]{:S(2)}) async-start(s8[6684672]{0:T(1024)(128)(4,1)} %bitcast.51), calls=%async_computation.6 | async-start | bytes 8388608
  172.4 4.3 %slice-start.3 = ((s8[6684672]{0:T(1024)(128)(4,1)}), s8[2490368]{0:T(1024)(128)(4,1)S(1)}, s32[]{:S(2)}) async-start(s8[6684672]{0:T(1024)(128)(4,1)} %bitcast.51), calls=%async_computation.7 | async-start | bytes 4980736
  180.0 8.3 %slice-start = ((s8[6684672]{0:T(1024)(128)(4,1)}), s8[4194304]{0:T(1024)(128)(4,1)S(1)}, s32[]{:S(2)}) async-start(s8[6684672]{0:T(1024)(128)(4,1)} %bitcast.49), calls=%async_computation.4 | async-start | bytes 8388608
  184.0 4.3 %slice-start.1 = ((s8[6684672]{0:T(1024)(128)(4,1)}), s8[2490368]{0:T(1024)(128)(4,1)S(1)}, s32[]{:S(2)}) async-start(s8[6684672]{0:T(1024)(128)(4,1)} %bitcast.49), calls=%async_computation.5 | async-start | bytes 4980736
  204.7 5.3 %copy-start.6 = (s32[192]{0:T(256)S(1)}, s32[192]{0:T(256)}, u32[]{:S(2)}) copy-start(s32[192]{0:T(256)} %param.12) | copy-start | bytes 2308
  204.7 5.3 %copy-start.5 = (f32[192]{0:T(256)S(1)}, f32[192]{0:T(256)}, u32[]{:S(2)}) copy-start(f32[192]{0:T(256)} %param.13) | copy-start | bytes 2308
  206.3 64.7 %all-to-all-start.3 = ((bf16[4,192,1024]{2,1,0:T(8,128)(2,1)}), bf16[4,192,1024]{2,1,0:T(8,128)(2,1)S(1)}, u32[]{:S(2)}, u32[]{:S(2)}) async-start(bf16[4,192,1024]{2,1,0:T(8,128)(2,1)} %bitcast.19), calls=%async_computation.3 | async-start | bytes 3145728 | tf_op jit(solution)/shard_map/all_to_all | solution.py:105
  270.5 1.8 copy-start.7
